TPU v7x, 128 devices: a whole 4x4x4 slice. The times are simulated.
128 devices in a mesh: gx: 4 (over x_lo, core), gy: 4 (over z), gz: 8 (over x_hi, y).
Axes of the slice: x: 4 (x_hi: 2, x_lo: 2; x = x_hi * 2 + x_lo), y: 4, z: 4, core: 2. Of those that a mesh axis runs over, the one named last changes fastest.
Arguments:
- fields: float32 [11, 500, 32, 1024], P(None, 'gx', 'gy', 'gz'), may hold values from -6 to 6
- var_scale: float32 [11], replicated, may hold values from 0.3 to 3
- start_basis: float32 [500, 64], replicated, may hold values from -6 to 6
Outputs:
- factor: float32 [500, 64], replicated
- core: float32 [64, 11, 32, 1024], P('gx', None, 'gy', 'gz')
All inputs are finite; a program needn't handle non-finite values.
Results may differ from a plain program's by a relative error of at most 0.0002.
Values sent between devices are 32-bit elements; how exact they have to be, the bound alone decides.
A program may use at most 128 MiB of HBM per device.

v0:
```python
import jax
import jax.numpy as jnp
from jax import lax
from jax.sharding import PartitionSpec as P

ITERS = 3


def orthonormal(block):
    small = jnp.dot(block.T, block, precision=lax.Precision.HIGHEST)
    lower = jnp.linalg.cholesky(small)
    return jax.scipy.linalg.solve_triangular(lower, block.T, lower=True).T


def per_device(fields, var_scale, start_basis):
    scaled = fields * var_scale[:, None, None, None]
    contract = (((0, 2, 3), (0, 2, 3)), ((), ()))
    swapped = lax.all_to_all(scaled, "gx", split_axis=2, concat_axis=1, tiled=True)
    partial_gram = lax.dot_general(swapped, swapped, contract, precision=lax.Precision.HIGHEST)
    gram = lax.psum(partial_gram, ("gx", "gy", "gz"))
    basis = start_basis
    for step in range(ITERS):
        basis = orthonormal(jnp.dot(gram, basis, precision=lax.Precision.HIGHEST))
    along_rows = (((0,), (1,)), ((), ()))
    full_core = lax.dot_general(basis, swapped, along_rows, precision=lax.Precision.HIGHEST)
    core = lax.all_to_all(full_core, "gx", split_axis=0, concat_axis=2, tiled=True)
    return (basis, core)


def solution(mesh):
    in_specs = (P(None, "gx", "gy", "gz"), P(), P())
    out_specs = (P(), P("gx", None, "gy", "gz"))
    return jax.shard_map(
        per_device, mesh=mesh, in_specs=in_specs, out_specs=out_specs, check_vma=False
    )
```

profile of v0, /device:TPU:1, one launch (start us, length us, event | category | flops | bytes accessed | tf_op | source)
XLA Modules:
  0.0 325.3 jit_solution(2125841500169065226)
XLA Ops:
  7.2 0.0 copy-start
  7.2 0.0 all-reduce.2.cloned.1.call-start
  7.2 3.1 broadcast_multiply_fusion
  10.3 1.1 copy.22
  11.4 68.0 %all_to_all.36 = f32[11,125,8,128]{3,1,0,2:T(8,128)S(1)} all-to-all(f32[11,125,8,128]{3,1,0,2:T(8,128)S(1)} %copy.22), channel_id=1, replica_groups=mesh['gx'=4,'gy'=4,'gz'=8] {'gx'}, dimensions={2} | all-to-all | bytes 11264000 | tf_op jit(solution)/shard_map/all_to_all | solution.py:18
  79.4 2.9 copy.32
  82.3 6.2 %all_to_all.29 = f32[11,500,2,128]{3,1,2,0:T(8,128)} reshape(f32[11,4,125,2,128]{4,2,1,3,0:T(8,128)} %bitcast.72) | data formatting | bytes 11264000 | tf_op jit(solution)/shard_map/all_to_all | solution.py:18
  88.5 13.6 %convolution_bitcast_fusion = f32[500,500]{1,0:T(8,128)} fusion(f32[11,500,2,128]{3,1,2,0:T(8,128)} %all_to_all.29), kind=kOutput, calls=%fused_computation.2 | convolution fusion | flops 8448000000 | bytes 6632000 | tf_op jit(solution)/shard_map/dot_general | solution.py:19
  102.1 0.0 all-reduce.2.cloned.1.call-update
  102.1 151.0 %all-reduce.2.cloned.1.call-done = f32[500,500]{1,0:T(8,128)} async-done(((f32[500,500]{1,0:T(8,128)}), f32[500,500]{1,0:T(8,128)}) %all-reduce.2.cloned.1.call-update) | async-done | bytes 1000016 | tf_op jit(solution)/shard_map/psum | solution.py:20
  253.1 0.0 copy-done
  253.1 2.3 fusion.21
  255.4 0.3 fusion.22
  255.7 0.1 copy.24
  255.7 5.8 %cholesky.59 = f32[64,64]{1,0:T(8,128)S(1)} custom-call(f32[64,64]{1,0:T(8,128)S(1)} %fusion.16), custom_call_target="Cholesky" | custom-call | tf_op jit(solution)/shard_map/jit(cholesky)/cholesky | solution.py:11
  261.6 0.6 compare_reduce_fusion.2
  262.3 0.7 fusion.8
  262.9 4.9 %custom-call.7 = f32[1,64,64]{1,2,0:T(8,128)S(1)} custom-call(f32[1,64,64]{2,1,0:T(8,128)S(1)} %fusion.8), custom_call_target="InvertDiagBlocksLowerTriangular" | custom-call | tf_op jit(solution)/shard_map/jit(_solve_triangular)/triangular_solve | solution.py:12
  267.8 0.3 fusion.6
  268.2 2.3 fusion.23
  270.5 0.3 fusion.24
  270.7 0.1 copy.25
  270.8 5.8 %cholesky.70 = f32[64,64]{1,0:T(8,128)S(1)} custom-call(f32[64,64]{1,0:T(8,128)S(1)} %fusion.14), custom_call_target="Cholesky" | custom-call | tf_op jit(solution)/shard_map/jit(cholesky)/cholesky | solution.py:11
  276.7 0.6 compare_reduce_fusion.1
  277.3 0.7 fusion.9
  278.0 4.9 %custom-call.8 = f32[1,64,64]{1,2,0:T(8,128)S(1)} custom-call(f32[1,64,64]{2,1,0:T(8,128)S(1)} %fusion.9), custom_call_target="InvertDiagBlocksLowerTriangular" | custom-call | tf_op jit(solution)/shard_map/jit(_solve_triangular)/triangular_solve | solution.py:12
  282.9 0.3 fusion.4
  283.2 2.3 fusion.25
  285.5 0.3 fusion.26
  285.8 0.1 copy.26
  285.9 5.8 %cholesky.81 = f32[64,64]{1,0:T(8,128)S(1)} custom-call(f32[64,64]{1,0:T(8,128)S(1)} %fusion.12), custom_call_target="Cholesky" | custom-call | tf_op jit(solution)/shard_map/jit(cholesky)/cholesky | solution.py:11
  291.8 0.6 compare_reduce_fusion
  292.4 0.7 fusion.10
  293.1 4.9 %custom-call.9 = f32[1,64,64]{1,2,0:T(8,128)S(1)} custom-call(f32[1,64,64]{2,1,0:T(8,128)S(1)} %fusion.10), custom_call_target="InvertDiagBlocksLowerTriangular" | custom-call | tf_op jit(solution)/shard_map/jit(_solve_triangular)/triangular_solve | solution.py:12
  298.0 0.3 fusion.2
  298.3 0.0 copy-start.1
  298.3 6.1 %fusion = f32[64,11,2,128]{3,0,2,1:T(8,128)S(1)} fusion(f32[11,500,2,128]{3,1,2,0:T(8,128)} %all_to_all.29, f32[64,500]{1,0:T(8,128)S(1)} %fusion.2), kind=kOutput, calls=%fused_computation.3 | convolution fusion | flops 1081344000 | bytes 6480896 | tf_op jit(solution)/shard_map/dot_general | solution.py:25
  304.5 0.6 copy.27
  305.0 12.3 %all_to_all.37 = f32[64,11,2,128]{3,2,1,0:T(2,128)S(1)} all-to-all(f32[64,11,2,128]{3,2,1,0:T(2,128)S(1)} %copy.27), channel_id=1, replica_groups=mesh['gx'=4,'gy'=4,'gz'=8] {'gx'}, dimensions={0} | all-to-all | bytes 1441792 | tf_op jit(solution)/shard_map/all_to_all | solution.py:26
  317.3 1.1 copy.28
  318.4 0.0 copy-done.1
  (6 shorter events, 0.1 us)
Async XLA Ops:
  7.2 245.9 %copy-start = (f32[500,64]{0,1:T(8,128)S(1)}, f32[500,64]{0,1:T(8,128)}, u32[]{:S(2)}) copy-start(f32[500,64]{0,1:T(8,128)} %param.8) | copy-start | bytes 384004
  7.2 245.9 %all-reduce.2.cloned.1.call-start = ((), (), s32[]{:S(2)}) async-start(), calls=%async_computation.2 | async-start | bytes 2064384 | tf_op jit(solution)/shard_map/psum | solution.py:20
  298.3 20.1 %copy-start.1 = (f32[64,500]{1,0:T(8,128)}, f32[64,500]{1,0:T(8,128)S(1)}, u32[]{:S(2)}) copy-start(f32[64,500]{1,0:T(8,128)S(1)} %fusion.2) | copy-start | bytes 384004
Sparse Core Ops, SparseCore 0:
  102.3 150.8 all-reduce.1
where the time goes:
time: 326 us; the launch traced here: 325 us
  waiting for transfers between devices  151 us (46%)
  blocking collectives  80.3 us (25%)
  other arithmetic  39.3 us (12%)
  matrix products  28.4 us (9%)
  between operations  14.2 us (4%)
  local copies, waits for them, and re-layouts  12.1 us (4%)
    psum x1, waiting for transfers between devices, per_device(): gram = lax.psum(partial_gram, ('gx', 'gy', 'gz'))  151 us
    all_to_all x1, blocking collectives, per_device(): lax.all_to_all(scaled, 'gx', split_axis=2, concat_axis=1, tiled=True)  68 us
    another operation x9, other arithmetic, orthonormal(): lower = jnp.linalg.cholesky(small)  19.6 us
    another operation x6, other arithmetic, orthonormal(): return jax.scipy.linalg.solve_triangular(lower, block.T, lower=True).T  16.6 us
    dot_general x1, matrix products, per_device(): lax.dot_general(swapped, swapped, contract, precision=lax.Precision.HIGHEST)  13.6 us
    all_to_all x1, blocking collectives, per_device(): lax.all_to_all(full_core, 'gx', split_axis=0, concat_axis=2, tiled=True)  12.3 us
    all_to_all x2, local copies, waits for them, and re-layouts, per_device(): lax.all_to_all(scaled, 'gx', split_axis=2, concat_axis=1, tiled=True)  9.05 us
    dot_general x3, matrix products, per_device(): basis = orthonormal(jnp.dot(gram, basis, precision=lax.Precision.HIGHEST))  6.83 us
  transfers between devices with their start and end apart: 1, of which 1 were waited for; matrix products, arithmetic and copies ran while one was open for 0% of the time, Pallas kernels for 0%

commit v1 on v0

--- a/solution.py
+++ b/solution.py
@@ -4,6 +4,12 @@
 from jax.sharding import PartitionSpec as P
 
 ITERS = 3
+
+
+def compute_forms_on(sheet):
+    all_rows = jax.lax.psum(sheet, ("gy", "gz"))
+    answer = jax.lax.psum(all_rows, "gx")
+    return answer
 
 
 def orthonormal(block):
@@ -17,7 +23,7 @@
     contract = (((0, 2, 3), (0, 2, 3)), ((), ()))
     swapped = lax.all_to_all(scaled, "gx", split_axis=2, concat_axis=1, tiled=True)
     partial_gram = lax.dot_general(swapped, swapped, contract, precision=lax.Precision.HIGHEST)
-    gram = lax.psum(partial_gram, ("gx", "gy", "gz"))
+    gram = compute_forms_on(partial_gram)
     basis = start_basis
     for step in range(ITERS):
         basis = orthonormal(jnp.dot(gram, basis, precision=lax.Precision.HIGHEST))

time: 326 us -> 577 us (1.77)
  waiting for transfers between devices: 151 us -> 401 us
    psum x1 -> x2, waiting for transfers between devices: 151 us -> 401 us  [the longest x1 335 us: compute_forms_on(): all_rows = jax.lax.psum(sheet, ('gy', 'gz'))]
  transfers between devices with their start and end apart: 1 -> 2, of which waited for: 1 -> 2; matrix products, arithmetic and copies ran while one was open for 0% -> 0% of each run, Pallas kernels for 0% -> 0%
where the time goes in v1:
time: 577 us; the launch traced here: 576 us
  waiting for transfers between devices  401 us (69%)
  blocking collectives  81 us (14%)
  other arithmetic  39.3 us (7%)
  matrix products  28.4 us (5%)
  between operations  14.2 us (2%)
  local copies, waits for them, and re-layouts  12.1 us (2%)
    psum x1, waiting for transfers between devices, compute_forms_on(): all_rows = jax.lax.psum(sheet, ('gy', 'gz'))  335 us
    all_to_all x1, blocking collectives, per_device(): lax.all_to_all(scaled, 'gx', split_axis=2, concat_axis=1, tiled=True)  68 us
    psum x1, waiting for transfers between devices, compute_forms_on(): answer = jax.lax.psum(all_rows, 'gx')  66.3 us
    another operation x9, other arithmetic, orthonormal(): lower = jnp.linalg.cholesky(small)  19.6 us
    another operation x6, other arithmetic, orthonormal(): return jax.scipy.linalg.solve_triangular(lower, block.T, lower=True).T  16.6 us
    dot_general x1, matrix products, per_device(): lax.dot_general(swapped, swapped, contract, precision=lax.Precision.HIGHEST)  13.6 us
    all_to_all x1, blocking collectives, per_device(): lax.all_to_all(full_core, 'gx', split_axis=0, concat_axis=2, tiled=True)  13 us
  transfers between devices with their start and end apart: 2, of which 2 were waited for; matrix products, arithmetic and copies ran while one was open for 0% of the time, Pallas kernels for 0%

profile of v1, /device:TPU:1, one launch (start us, length us, event | category | flops | bytes accessed | tf_op | source)
XLA Modules:
  0.0 576.1 jit_solution(7991892348294177944)
XLA Ops:
  7.2 0.0 copy-start
  7.2 0.0 all-reduce.3.cloned.1.call-start
  7.2 3.1 broadcast_multiply_fusion
  10.3 1.1 copy.22
  11.4 68.0 %all_to_all.36 = f32[11,125,8,128]{3,1,0,2:T(8,128)S(1)} all-to-all(f32[11,125,8,128]{3,1,0,2:T(8,128)S(1)} %copy.22), channel_id=1, replica_groups=mesh['gx'=4,'gy'=4,'gz'=8] {'gx'}, dimensions={2} | all-to-all | bytes 11264000 | tf_op jit(solution)/shard_map/all_to_all | solution.py:24
  79.4 2.9 copy.32
  82.3 6.2 %all_to_all.29 = f32[11,500,2,128]{3,1,2,0:T(8,128)} reshape(f32[11,4,125,2,128]{4,2,1,3,0:T(8,128)} %bitcast.72) | data formatting | bytes 11264000 | tf_op jit(solution)/shard_map/all_to_all | solution.py:24
  88.5 13.6 %convolution_bitcast_fusion = f32[500,500]{1,0:T(8,128)} fusion(f32[11,500,2,128]{3,1,2,0:T(8,128)} %all_to_all.29), kind=kOutput, calls=%fused_computation.2 | convolution fusion | flops 8448000000 | bytes 6632000 | tf_op jit(solution)/shard_map/dot_general | solution.py:25
  102.1 0.0 all-reduce.3.cloned.1.call-update
  102.1 0.2 all-reduce.5.cloned.1.call-start
  102.4 334.6 %all-reduce.3.cloned.1.call-done = f32[500,500]{1,0:T(8,128)} async-done(((f32[500,500]{1,0:T(8,128)}), f32[500,500]{1,0:T(8,128)}) %all-reduce.3.cloned.1.call-update) | async-done | bytes 1000016 | tf_op jit(solution)/shard_map/psum | solution.py:10
  437.0 0.0 all-reduce.5.cloned.1.call-update
  437.0 66.3 %all-reduce.5.cloned.1.call-done = f32[500,500]{1,0:T(8,128)} async-done(((f32[500,500]{1,0:T(8,128)}), f32[500,500]{1,0:T(8,128)}) %all-reduce.5.cloned.1.call-update) | async-done | bytes 1000016 | tf_op jit(solution)/shard_map/psum | solution.py:11
  503.3 0.0 copy-done
  503.3 2.3 fusion.21
  505.6 0.3 fusion.22
  505.9 0.1 copy.24
  506.0 5.8 %cholesky.59 = f32[64,64]{1,0:T(8,128)S(1)} custom-call(f32[64,64]{1,0:T(8,128)S(1)} %fusion.16), custom_call_target="Cholesky" | custom-call | tf_op jit(solution)/shard_map/jit(cholesky)/cholesky | solution.py:17
  511.9 0.6 compare_reduce_fusion.2
  512.5 0.7 fusion.8
  513.2 4.9 custom-call.7
  518.1 0.3 fusion.6
  518.4 2.3 fusion.23
  520.7 0.3 fusion.24
  520.9 0.1 copy.25
  521.0 5.8 %cholesky.70 = f32[64,64]{1,0:T(8,128)S(1)} custom-call(f32[64,64]{1,0:T(8,128)S(1)} %fusion.14), custom_call_target="Cholesky" | custom-call | tf_op jit(solution)/shard_map/jit(cholesky)/cholesky | solution.py:17
  526.9 0.6 compare_reduce_fusion.1
  527.6 0.7 fusion.9
  528.2 4.9 custom-call.8
  533.1 0.3 fusion.4
  533.5 2.3 fusion.25
  535.8 0.3 fusion.26
  536.0 0.1 copy.26
  536.1 5.8 %cholesky.81 = f32[64,64]{1,0:T(8,128)S(1)} custom-call(f32[64,64]{1,0:T(8,128)S(1)} %fusion.12), custom_call_target="Cholesky" | custom-call | tf_op jit(solution)/shard_map/jit(cholesky)/cholesky | solution.py:17
  542.0 0.6 compare_reduce_fusion
  542.6 0.7 fusion.10
  543.3 4.9 custom-call.9
  548.2 0.3 fusion.2
  548.5 0.0 copy-start.1
  548.6 6.1 %fusion = f32[64,11,2,128]{3,0,2,1:T(8,128)S(1)} fusion(f32[11,500,2,128]{3,1,2,0:T(8,128)} %all_to_all.29, f32[64,500]{1,0:T(8,128)S(1)} %fusion.2), kind=kOutput, calls=%fused_computation.3 | convolution fusion | flops 1081344000 | bytes 6480896 | tf_op jit(solution)/shard_map/dot_general | solution.py:31
  554.7 0.6 copy.27
  555.2 13.0 %all_to_all.37 = f32[64,11,2,128]{3,2,1,0:T(2,128)S(1)} all-to-all(f32[64,11,2,128]{3,2,1,0:T(2,128)S(1)} %copy.27), channel_id=1, replica_groups=mesh['gx'=4,'gy'=4,'gz'=8] {'gx'}, dimensions={0} | all-to-all | bytes 1441792 | tf_op jit(solution)/shard_map/all_to_all | solution.py:32
  568.2 1.1 copy.28
  569.3 0.0 copy-done.1
  (6 shorter events, 0.1 us)
Async XLA Ops:
  7.2 496.2 %copy-start = (f32[500,64]{0,1:T(8,128)S(1)}, f32[500,64]{0,1:T(8,128)}, u32[]{:S(2)}) copy-start(f32[500,64]{0,1:T(8,128)} %param.8) | copy-start | bytes 384004
  7.2 429.8 %all-reduce.3.cloned.1.call-start = ((), (), s32[]{:S(2)}) async-start(), calls=%async_computation.2 | async-start | bytes 2064384 | tf_op jit(solution)/shard_map/psum | solution.py:10
  102.1 401.2 %all-reduce.5.cloned.1.call-start = ((), (), s32[]{:S(2)}) async-start(), calls=%async_computation.3 | async-start | bytes 2064384 | tf_op jit(solution)/shard_map/psum | solution.py:11
  548.5 20.8 %copy-start.1 = (f32[64,500]{1,0:T(8,128)}, f32[64,500]{1,0:T(8,128)S(1)}, u32[]{:S(2)}) copy-start(f32[64,500]{1,0:T(8,128)S(1)} %fusion.2) | copy-start | bytes 384004
Sparse Core Ops, SparseCore 0:
  102.3 334.6 all-reduce.2
  439.5 63.7 all-reduce.4

commit v2 on v0

--- a/solution.py
+++ b/solution.py
@@ -15,7 +15,15 @@
 def per_device(fields, var_scale, start_basis):
     scaled = fields * var_scale[:, None, None, None]
     contract = (((0, 2, 3), (0, 2, 3)), ((), ()))
-    swapped = lax.all_to_all(scaled, "gx", split_axis=2, concat_axis=1, tiled=True)
+    swapped = jnp.concatenate(
+        lax.all_to_all(
+            jnp.stack(jnp.split(scaled, lax.axis_size("gx"), 2), axis=0),
+            axis_name="gx",
+            concat_axis=0,
+            split_axis=0,
+        ),
+        1,
+    )
     partial_gram = lax.dot_general(swapped, swapped, contract, precision=lax.Precision.HIGHEST)
     gram = lax.psum(partial_gram, ("gx", "gy", "gz"))
     basis = start_basis

time: 326 us -> 329 us (level)
    reshape x0 -> x2, local copies, waits for them, and re-layouts: none -> 9.44 us  [per_device(): jnp.concatenate(lax.all_to_all(jnp.stack(jnp.split(scaled, lax.axis_size(...]
    all_to_all x2 -> x0, local copies, waits for them, and re-layouts: 9.05 us -> none  [per_device(): lax.all_to_all(scaled, 'gx', split_axis=2, concat_axis=1, tiled=True)]
where the time goes in v2:
time: 329 us; the launch traced here: 328 us
  waiting for transfers between devices  151 us (46%)
  blocking collectives  78.8 us (24%)
  other arithmetic  42.3 us (13%)
  matrix products  28.4 us (9%)
  between operations  14.2 us (4%)
  local copies, waits for them, and re-layouts  13.4 us (4%)
    psum x1, waiting for transfers between devices, per_device(): gram = lax.psum(partial_gram, ('gx', 'gy', 'gz'))  151 us
    all_to_all x1, blocking collectives, per_device(): lax.all_to_all(jnp.stack(jnp.split(scaled, lax.axis_size('gx'), 2), axis=...  66.6 us
    another operation x9, other arithmetic, orthonormal(): lower = jnp.linalg.cholesky(small)  19.6 us
    another operation x6, other arithmetic, orthonormal(): return jax.scipy.linalg.solve_triangular(lower, block.T, lower=True).T  16.6 us
    dot_general x1, matrix products, per_device(): lax.dot_general(swapped, swapped, contract, precision=lax.Precision.HIGHEST)  13.6 us
    all_to_all x1, blocking collectives, per_device(): lax.all_to_all(full_core, 'gx', split_axis=0, concat_axis=2, tiled=True)  12.3 us
    reshape x2, local copies, waits for them, and re-layouts, per_device(): jnp.concatenate(lax.all_to_all(jnp.stack(jnp.split(scaled, lax.axis_size(...  9.44 us
    dot_general x3, matrix products, per_device(): basis = orthonormal(jnp.dot(gram, basis, precision=lax.Precision.HIGHEST))  6.83 us
  transfers between devices with their start and end apart: 1, of which 1 were waited for; matrix products, arithmetic and copies ran while one was open for 0% of the time, Pallas kernels for 0%

profile of v2, /device:TPU:1, one launch (start us, length us, event | category | flops | bytes accessed | tf_op | source)
XLA Modules:
  0.0 328.1 jit_solution(1241575874143370499)
XLA Ops:
  7.2 0.0 copy-start
  7.2 0.0 all-reduce.2.cloned.1.call-start
  7.2 3.1 broadcast_multiply_fusion
  10.3 2.0 slice_bitcast_fusion.3
  12.3 3.0 pad_maximum_fusion
  15.3 66.6 %all_to_all.23 = f32[4,11,125,2,128]{4,3,2,1,0:T(2,128)S(1)} all-to-all(f32[4,11,125,2,128]{4,3,2,1,0:T(2,128)S(1)} %pad_maximum_fusion), channel_id=1, replica_groups=mesh['gx'=4,'gy'=4,'gz'=8] {'gx'}, dimensions={0} | all-to-all | bytes 11264000 | tf_op jit(solution)/shard_map/all_to_all | solution.py:19
  81.9 3.3 copy.15
  85.1 6.2 %reshape.20 = f32[11,500,2,128]{3,1,2,0:T(8,128)} reshape(f32[11,4,125,2,128]{4,2,1,3,0:T(8,128)} %copy.15) | data formatting | bytes 11264000 | tf_op jit(solution)/shard_map/reshape | solution.py:18
  91.3 13.6 %convolution_bitcast_fusion = f32[500,500]{1,0:T(8,128)} fusion(f32[11,500,2,128]{3,1,2,0:T(8,128)} %reshape.20), kind=kOutput, calls=%fused_computation.6 | convolution fusion | flops 8448000000 | bytes 6632000 | tf_op jit(solution)/shard_map/dot_general | solution.py:27
  105.0 0.0 all-reduce.2.cloned.1.call-update
  105.0 150.9 %all-reduce.2.cloned.1.call-done = f32[500,500]{1,0:T(8,128)} async-done(((f32[500,500]{1,0:T(8,128)}), f32[500,500]{1,0:T(8,128)}) %all-reduce.2.cloned.1.call-update) | async-done | bytes 1000016 | tf_op jit(solution)/shard_map/psum | solution.py:28
  255.9 0.0 copy-done
  255.9 2.3 fusion.21
  258.2 0.3 fusion.22
  258.5 0.1 copy.16
  258.6 5.8 %cholesky.59 = f32[64,64]{1,0:T(8,128)S(1)} custom-call(f32[64,64]{1,0:T(8,128)S(1)} %fusion.16), custom_call_target="Cholesky" | custom-call | tf_op jit(solution)/shard_map/jit(cholesky)/cholesky | solution.py:11
  264.4 0.6 compare_reduce_fusion.2
  265.1 0.7 fusion.8
  265.7 4.9 %custom-call.7 = f32[1,64,64]{1,2,0:T(8,128)S(1)} custom-call(f32[1,64,64]{2,1,0:T(8,128)S(1)} %fusion.8), custom_call_target="InvertDiagBlocksLowerTriangular" | custom-call | tf_op jit(solution)/shard_map/jit(_solve_triangular)/triangular_solve | solution.py:12
  270.6 0.3 fusion.6
  271.0 2.3 fusion.23
  273.3 0.3 fusion.24
  273.5 0.1 copy.17
  273.6 5.8 %cholesky.70 = f32[64,64]{1,0:T(8,128)S(1)} custom-call(f32[64,64]{1,0:T(8,128)S(1)} %fusion.14), custom_call_target="Cholesky" | custom-call | tf_op jit(solution)/shard_map/jit(cholesky)/cholesky | solution.py:11
  279.5 0.6 compare_reduce_fusion.1
  280.2 0.7 fusion.9
  280.8 4.9 %custom-call.8 = f32[1,64,64]{1,2,0:T(8,128)S(1)} custom-call(f32[1,64,64]{2,1,0:T(8,128)S(1)} %fusion.9), custom_call_target="InvertDiagBlocksLowerTriangular" | custom-call | tf_op jit(solution)/shard_map/jit(_solve_triangular)/triangular_solve | solution.py:12
  285.7 0.3 fusion.4
  286.1 2.3 fusion.25
  288.3 0.3 fusion.26
  288.6 0.1 copy.18
  288.7 5.8 %cholesky.81 = f32[64,64]{1,0:T(8,128)S(1)} custom-call(f32[64,64]{1,0:T(8,128)S(1)} %fusion.12), custom_call_target="Cholesky" | custom-call | tf_op jit(solution)/shard_map/jit(cholesky)/cholesky | solution.py:11
  294.6 0.6 compare_reduce_fusion
  295.2 0.7 fusion.10
  295.9 4.9 %custom-call.9 = f32[1,64,64]{1,2,0:T(8,128)S(1)} custom-call(f32[1,64,64]{2,1,0:T(8,128)S(1)} %fusion.10), custom_call_target="InvertDiagBlocksLowerTriangular" | custom-call | tf_op jit(solution)/shard_map/jit(_solve_triangular)/triangular_solve | solution.py:12
  300.8 0.3 fusion.2
  301.1 0.0 copy-start.1
  301.1 6.1 %fusion = f32[64,11,2,128]{3,0,2,1:T(8,128)S(1)} fusion(f32[11,500,2,128]{3,1,2,0:T(8,128)} %reshape.20, f32[64,500]{1,0:T(8,128)S(1)} %fusion.2), kind=kOutput, calls=%fused_computation.7 | convolution fusion | flops 1081344000 | bytes 6480896 | tf_op jit(solution)/shard_map/dot_general | solution.py:33
  307.3 0.6 copy.19
  307.8 12.3 %all_to_all.24 = f32[64,11,2,128]{3,2,1,0:T(2,128)S(1)} all-to-all(f32[64,11,2,128]{3,2,1,0:T(2,128)S(1)} %copy.19), channel_id=1, replica_groups=mesh['gx'=4,'gy'=4,'gz'=8] {'gx'}, dimensions={0} | all-to-all | bytes 1441792 | tf_op jit(solution)/shard_map/all_to_all | solution.py:34
  320.1 1.1 copy.20
  321.2 0.0 copy-done.1
  (6 shorter events, 0.1 us)
Async XLA Ops:
  7.2 248.8 %copy-start = (f32[500,64]{0,1:T(8,128)S(1)}, f32[500,64]{0,1:T(8,128)}, u32[]{:S(2)}) copy-start(f32[500,64]{0,1:T(8,128)} %param.8) | copy-start | bytes 384004
  7.2 248.7 %all-reduce.2.cloned.1.call-start = ((), (), s32[]{:S(2)}) async-start(), calls=%async_computation.2 | async-start | bytes 2064384 | tf_op jit(solution)/shard_map/psum | solution.py:28
  301.1 20.1 %copy-start.1 = (f32[64,500]{1,0:T(8,128)}, f32[64,500]{1,0:T(8,128)S(1)}, u32[]{:S(2)}) copy-start(f32[64,500]{1,0:T(8,128)S(1)} %fusion.2) | copy-start | bytes 384004
Sparse Core Ops, SparseCore 0:
  105.1 150.7 all-reduce.1
